TPU v7x, 256 devices: a whole 4x4x8 slice. The times are simulated.
256 devices in a mesh: view: 8 (over x, core), gauss: 32 (over y, z).
Axes of the slice: x: 4, y: 4, z: 8, core: 2. Of those that a mesh axis runs over, the one named last changes fastest.
Arguments:
- means: float32 [3, 524288], P(None, 'gauss'), may hold values from -1 to 1
- scales: float32 [3, 524288], P(None, 'gauss'), may hold values from 0.05 to 0.6
- quats: float32 [4, 524288], P(None, 'gauss'), may hold values from -6 to 6
- attrs: float32 [49, 524288], P(None, 'gauss'), may hold values from -6 to 6
- grad_screen: float32 [32, 2, 524288], P('view', None, 'gauss'), may hold values from -6 to 6
- visible: int32 [32, 524288], P('view', 'gauss'), may hold values 0 or 1
- clone_mask: int32 [524288], P('gauss'), may hold values from 0 to 1, as said below
- rotation: float32 [32, 3, 3], P('view'), may hold values from -3.5 to 3.5
- shift: float32 [32, 3], P('view'), may hold values from 2 to 5
- focal: float32 [32], P('view'), may hold values from 1 to 4
Outputs:
- peak_stats: float32 [2, 524288], P(None, 'gauss')
- clones: float32 [61, 524288], P(None, 'gauss')
- clone_total: int32 [], replicated
Inputs may be any that keep to these rules, and one draw needn't show every extreme that they name: `clone_mask`: in every draw some shard of 16384 consecutive Gaussians has all of them marked.
All inputs are finite; a program needn't handle non-finite values. No bound on the sum of `visible` on one device may be relied on, other than what follows from the above.
Results may differ from a plain program's by a relative error of at most 0.0003.
Values sent between devices are 32-bit elements; how exact they have to be, the bound alone decides.
A program may use at most 128 MiB of HBM per device.

v0:
```python
import functools

import jax
import jax.numpy as jnp
from jax import lax
from jax.experimental import pallas as pl
from jax.experimental.pallas import tpu as pltpu
from jax.sharding import PartitionSpec as P

LANES = 128
SUB = 8
ATTR_TILES = 6
TILES = ATTR_TILES + 2
VMEM = pltpu.VMEM
SMEM = pltpu.SMEM
MESH = pl.DeviceIdType.MESH


def spec(space):
    return pl.BlockSpec(memory_space=space)


def peer(view, gauss):
    return {"view": view, "gauss": gauss}


def quat_factor(scales, quats):
    w, x, y, z = quats
    inv = 1.0 / jnp.sqrt(w * w + x * x + y * y + z * z + 0.25)
    w, x, y, z = (w * inv, x * inv, y * inv, z * inv)
    rq = [
        [1 - 2 * (y * y + z * z), 2 * (x * y - w * z), 2 * (x * z + w * y)],
        [2 * (x * y + w * z), 1 - 2 * (x * x + z * z), 2 * (y * z - w * x)],
        [2 * (x * z - w * y), 2 * (y * z + w * x), 1 - 2 * (x * x + y * y)],
    ]
    return [[rq[i][j] * scales[j] for j in range(3)] for i in range(3)]


def view_radius(means, factor, rot, trans, focal_v):
    point = [
        rot[i][0] * means[0] + rot[i][1] * means[1] + rot[i][2] * means[2] + trans[i]
        for i in range(3)
    ]
    inv = 1.0 / jnp.maximum(point[2], 1.0)
    j00 = focal_v * inv
    j02 = -(j00 * point[0]) * inv
    j12 = -(j00 * point[1]) * inv
    first = [j00 * rot[0][j] + j02 * rot[2][j] for j in range(3)]
    second = [j00 * rot[1][j] + j12 * rot[2][j] for j in range(3)]
    prow = [sum((first[j] * factor[j][k] for j in range(3))) for k in range(3)]
    qrow = [sum((second[j] * factor[j][k] for j in range(3))) for k in range(3)]
    a_val = prow[0] * prow[0] + prow[1] * prow[1] + prow[2] * prow[2] + 0.3
    c_val = qrow[0] * qrow[0] + qrow[1] * qrow[1] + qrow[2] * qrow[2] + 0.3
    b_val = prow[0] * qrow[0] + prow[1] * qrow[1] + prow[2] * qrow[2]
    half = 0.5 * (a_val - c_val)
    lam = 0.5 * (a_val + c_val) + jnp.sqrt(half * half + b_val * b_val + 0.01)
    return 3.0 * jnp.sqrt(lam)


def stats_kernel(
    V, S, views, rots, trns, foc, mask, means, scales, quats, grad, vis, peak, meta,
    cnt, counts, local, halves, merged, whole, total_max,
    csend, crecv, rsend, rrecv, gsend, grecv,
):
    v, s = lax.axis_index("view"), lax.axis_index("gauss")
    nblk = mask.shape[0]
    piece = 2 * nblk // V
    cnt[...] = jnp.full((SUB, LANES), jnp.sum(mask[...]), jnp.int32)
    bar = pltpu.get_barrier_semaphore()
    for k in range(1, S):
        pl.semaphore_signal(bar, inc=1, device_id=peer(v, lax.rem(s + k, S)), device_id_type=MESH)
    for k in range(1, V):
        pl.semaphore_signal(bar, inc=1, device_id=peer(lax.rem(v + k, V), s), device_id_type=MESH)

    step = 2 * SUB

    def chunk(i, carry):
        rows = pl.ds(pl.multiple_of(i * step, step), step)

        def lines(ref, count, c):
            return ref[pl.ds(i * step * count + c, step, stride=count), :]

        m = [means[rows, c, :] for c in range(3)]
        factor = quat_factor(
            [scales[rows, c, :] for c in range(3)], [lines(quats, 4, c) for c in range(4)]
        )
        gmax = jnp.zeros((step, LANES), jnp.float32)
        rmax = jnp.zeros((step, LANES), jnp.float32)
        for u in range(views):
            rot = [[rots[u, a, b] for b in range(3)] for a in range(3)]
            trans = [trns[u, a] for a in range(3)]
            radius = view_radius(m, factor, rot, trans, foc[u])
            seen = lines(vis, views, u).astype(jnp.float32)
            g0, g1 = (grad[u, pl.ds(i * step * 2 + c, step, stride=2), :] for c in range(2))
            gmax = jnp.maximum(gmax, jnp.sqrt(g0 * g0 + g1 * g1) * seen)
            rmax = jnp.maximum(rmax, radius * seen)
        local[pl.ds(i * step * 2, step, stride=2), :] = gmax
        local[pl.ds(i * step * 2 + 1, step, stride=2), :] = rmax
        return carry

    lax.fori_loop(0, nblk // step, chunk, 0)
    pl.semaphore_wait(bar, S + V - 2)
    copies = []
    for k in range(1, V):
        to = lax.rem(v + k, V)
        rs = pltpu.make_async_remote_copy(
            src_ref=local.at[pl.ds(pl.multiple_of(to * piece, piece), piece), :],
            dst_ref=halves.at[k],
            send_sem=rsend.at[k],
            recv_sem=rrecv.at[k],
            device_id=peer(to, s),
            device_id_type=MESH,
        )
        rs.start()
        copies.append(rs)
    tally = []
    for k in range(1, S):
        cp = pltpu.make_async_remote_copy(
            src_ref=cnt,
            dst_ref=counts.at[k],
            send_sem=csend.at[k],
            recv_sem=crecv.at[k],
            device_id=peer(v, lax.rem(s + k, S)),
            device_id_type=MESH,
        )
        cp.start()
        tally.append(cp)
    for rs in copies:
        rs.wait_recv()
    mine = pl.ds(pl.multiple_of(v * piece, piece), piece)
    best = local[mine, :]
    for k in range(1, V):
        best = jnp.maximum(best, halves[k])
    merged[...] = best
    spread = []
    for k in range(1, V):
        ag = pltpu.make_async_remote_copy(
            src_ref=merged,
            dst_ref=whole.at[k],
            send_sem=gsend.at[k],
            recv_sem=grecv.at[k],
            device_id=peer(lax.rem(v + k, V), s),
            device_id_type=MESH,
        )
        ag.start()
        spread.append(ag)
    for cp in tally:
        cp.wait_recv()
    lane = lax.broadcasted_iota(jnp.int32, (SUB, LANES), 1)
    sub = lax.broadcasted_iota(jnp.int32, (SUB, LANES), 0)
    blocks = jnp.zeros((SUB, LANES), jnp.int32)
    offs = jnp.zeros((SUB, LANES), jnp.int32)
    total = jnp.zeros((SUB, LANES), jnp.int32)
    for k in range(S):
        c = cnt[...] if k == 0 else counts[k]
        who = lax.rem(s + S - k, S)
        b = (c + (LANES - 1)) // LANES
        blocks = jnp.where(lane == who, b, blocks)
        offs = offs + jnp.where(lane > who, b, 0)
        total = total + c
    meta[...] = jnp.where(sub == 0, blocks, jnp.where(sub == 1, offs, total))
    total_max[mine, :] = best
    for k in range(1, V):
        spread[k - 1].wait_recv()
        who = lax.rem(v + V - k, V)
        total_max[pl.ds(pl.multiple_of(who * piece, piece), piece), :] = whole[k]
    for c in range(2):
        peak[:, c, :] = total_max[pl.ds(c, nblk, stride=2), :]
    for cp in copies + tally + spread:
        cp.wait_send()


def pack_kernel(
    V, S, T, per, meta, mask, attrs, means, scales, quats, peak, out,
    x, enc, basev, bases, sem, sem2,
):
    v, s = lax.axis_index("view"), lax.axis_index("gauss")
    nblk = mask.shape[0]
    for j in range(T):
        tile = v * T + j

        @pl.when(tile < ATTR_TILES)
        def _():
            pltpu.make_async_copy(
                attrs.at[pl.ds(pl.multiple_of(tile * SUB, SUB), SUB), :], x.at[j], sem.at[j]
            ).start()

        @pl.when(tile == ATTR_TILES + 1)
        def _():
            pltpu.make_async_copy(
                attrs.at[pl.ds(ATTR_TILES * SUB, 1), :], x.at[j, pl.ds(2, 1), :], sem.at[j]
            ).start()

    m = mask[...]
    lane = lax.broadcasted_iota(jnp.int32, (nblk, LANES), 1)
    mb = m.astype(jnp.bfloat16)
    li = lax.broadcasted_iota(jnp.int32, (LANES, LANES), 0)
    lj = lax.broadcasted_iota(jnp.int32, (LANES, LANES), 1)
    before = (li < lj).astype(jnp.bfloat16)
    bi = lax.broadcasted_iota(jnp.int32, (nblk, nblk), 0)
    bj = lax.broadcasted_iota(jnp.int32, (nblk, nblk), 1)
    above = (bi > bj).astype(jnp.bfloat16)
    under = (bi < bj).astype(jnp.bfloat16)
    dot = functools.partial(jnp.dot, preferred_element_type=jnp.float32)
    ones = jnp.ones((LANES, LANES), jnp.bfloat16)
    rank = dot(mb, before).astype(jnp.int32)
    size = dot(mb, ones).astype(jnp.int32)
    base = dot(dot(above, mb).astype(jnp.bfloat16), ones).astype(jnp.int32)
    flat = lax.dot_general(
        jnp.ones((SUB, LANES), jnp.bfloat16), mb, (((1,), (1,)), ((), ())),
        preferred_element_type=jnp.float32,
    )
    starts = dot(flat.astype(jnp.bfloat16), under)
    top = lax.broadcasted_iota(jnp.int32, (SUB, nblk), 0) == 0
    basev[...] = jnp.where(top, starts, starts + flat).astype(jnp.int32)
    scal = pltpu.make_async_copy(basev, bases, sem2)
    scal.start()
    code = jnp.where(m == 1, 65536 + (lane - rank) * 256 + lane, 0)
    bit = 1
    while bit < LANES:
        moved = pltpu.roll(code, LANES - bit, 1)
        goes = (moved & (bit * 256)) != 0
        stays = (code & (bit * 256)) == 0
        code = jnp.where(goes, moved, jnp.where(stays, code, 0))
        bit *= 2
    turn = (lane - base) & (LANES - 1)
    src = jnp.take_along_axis(code & (LANES - 1), turn, axis=1)
    enc[...] = jnp.where(turn < size, src, -1)

    for j in range(T):
        tile = v * T + j

        @pl.when(tile == ATTR_TILES)
        def _():
            x[j, 0:3, :] = means[...]
            x[j, 3:6, :] = scales[...]
            x[j, 6:8, :] = quats[0:2, :]

        @pl.when(tile == ATTR_TILES + 1)
        def _():
            x[j, 0:2, :] = quats[2:4, :]
            x[j, 3:5, :] = peak[...]
            x[j, 5:8, :] = jnp.zeros((3, peak.shape[1]), jnp.float32)
            pltpu.make_async_copy(
                attrs.at[pl.ds(ATTR_TILES * SUB, 1), :], x.at[j, pl.ds(2, 1), :], sem.at[j]
            ).wait()

        @pl.when(tile < ATTR_TILES)
        def _():
            pltpu.make_async_copy(attrs.at[pl.ds(0, SUB), :], x.at[j], sem.at[j]).wait()

    out[...] = jnp.zeros_like(out)
    scal.wait()
    offset = meta[1, s]
    row = lax.broadcasted_iota(jnp.int32, (SUB, LANES), 1)

    def spot(d):
        return jnp.where(d < nblk, lax.rem(offset + d, S) * per + lax.div(d, S), S * per)

    def move(b, cur):
        start = bases[0, b]
        off = lax.rem(start, LANES)
        d = lax.div(start, LANES)
        e = jnp.broadcast_to(enc[pl.ds(b, 1), :], (SUB, LANES))
        idx = jnp.maximum(e, 0)
        ok = e >= 0
        low = ok & (row >= off)
        high = ok & (row < off)
        where = spot(d)
        cols = pl.ds(pl.multiple_of(b * LANES, LANES), LANES)
        full = bases[1, b] >= (d + 1) * LANES
        nxt = []
        for j in range(T):
            g = jnp.take_along_axis(x[j, :, cols], idx, axis=1)
            keep = jnp.where(low, g, cur[j])
            out[where, j * SUB:(j + 1) * SUB, :] = keep
            nxt.append(jnp.where(full, jnp.where(high, g, 0.0), keep))
        return tuple(nxt)

    zero = jnp.zeros((SUB, LANES), jnp.float32)
    cur = lax.fori_loop(0, nblk, move, (zero,) * T, unroll=8)
    end = lax.div(bases[1, nblk - 1], LANES)
    for j in range(T):
        out[spot(end), j * SUB:(j + 1) * SUB, :] = cur[j]


def pair(s, k, S):
    if S & (S - 1):
        return lax.rem(s + k, S), lax.rem(s + S - k, S)
    t, bit = s, 1
    while bit < S:
        if k & bit:
            t = t + bit * (1 - 2 * lax.rem(lax.div(s, bit), 2))
        bit *= 2
    return t, t


def ship_kernel(V, S, per, src, buf, gsend, vsend, csend, recv, lsem):
    v, s = lax.axis_index("view"), lax.axis_index("gauss")
    core = lax.rem(v, 2)
    mate = v + 1 - 2 * core
    X = V // 2
    bar = pltpu.get_barrier_semaphore()
    for k in range(1, S):
        pl.semaphore_signal(bar, inc=1, device_id=peer(v, lax.rem(s + k, S)), device_id_type=MESH)
    for q in range(1, X):
        pl.semaphore_signal(
            bar, inc=1, device_id=peer(lax.rem(v + 2 * q, V), s), device_id_type=MESH
        )
    pl.semaphore_signal(bar, inc=1, device_id=peer(mate, s), device_id_type=MESH)
    pl.semaphore_wait(bar, S - 1 + X)

    def part(i):
        return pl.ds(i * per, per)

    def far(k):
        to = pair(s, k, S)[0]
        return pltpu.make_async_remote_copy(
            src_ref=src.at[part(to)], dst_ref=buf.at[v, part(s)],
            send_sem=gsend.at[k], recv_sem=recv.at[0, k],
            device_id=peer(v, to), device_id_type=MESH,
        )

    def at(k, q):
        owner = lax.rem(v + V - 2 * q, V)
        frm = pair(s, k, S)[1]
        if k == 0 and q == 0:
            return src.at[part(s)], owner, frm
        return buf.at[owner, part(frm)], owner, frm

    def across(k, q):
        ref, _, frm = at(k, 0)
        return pltpu.make_async_remote_copy(
            src_ref=ref, dst_ref=buf.at[v, part(frm)],
            send_sem=vsend.at[q, k], recv_sem=recv.at[q, k],
            device_id=peer(lax.rem(v + 2 * q, V), s), device_id_type=MESH,
        )

    def beside(k, q):
        ref, owner, frm = at(k, q)
        return pltpu.make_async_remote_copy(
            src_ref=ref, dst_ref=buf.at[owner, part(frm)],
            send_sem=csend.at[q, k], recv_sem=recv.at[X + q, k],
            device_id=peer(mate, s), device_id_type=MESH,
        )

    started = []

    def go(copy):
        copy.start()
        started.append(copy)

    fars = {k: far(k) for k in range(1, S)}
    for k in range(1, S):
        go(fars[k])
    for q in range(1, X):
        go(across(0, q))
    go(beside(0, 0))
    own = pltpu.make_async_copy(src.at[part(s)], buf.at[v, part(s)], lsem)
    own.start()
    for k in range(S):
        if k:
            fars[k].wait_recv()
            for q in range(1, X):
                go(across(k, q))
            go(beside(k, 0))
        if k:
            for q in range(1, X):
                across(k - 1, q).wait_recv()
                go(beside(k - 1, q))
    for q in range(1, X):
        across(S - 1, q).wait_recv()
        go(beside(S - 1, q))
    for k in range(S):
        for q in range(X):
            beside(k, q).wait_recv()
    for copy in started:
        copy.wait_send()
    own.wait()


def place_kernel(S, T, per, meta, buf, out):
    me = lax.axis_index("gauss")
    slots = out.shape[1] // LANES
    sub = lax.broadcasted_iota(jnp.int32, (SUB, LANES), 0)
    rows = out.shape[0]
    head = sub < 2
    filled = jnp.int32(0)
    for s in range(S):
        blocks, offset = meta[0, s], meta[1, s]
        first = lax.rem(me + S - lax.rem(offset, S), S)
        n = lax.div(jnp.maximum(blocks - first, 0) + (S - 1), S)
        slot0 = lax.div(offset + first, S)

        def one(w, carry):
            t = []
            for tile in range(TILES):
                j = tile % T
                t.append(buf[tile // T, s * per + w, j * SUB:(j + 1) * SUB, :])
            turned = [pltpu.roll(a, 2, 0) for a in t[:ATTR_TILES]]
            mixed = t[ATTR_TILES + 1]
            chain = [mixed] + turned + [mixed]
            cols = pl.ds(pl.multiple_of((slot0 + w) * LANES, LANES), LANES)
            out[0:SUB, cols] = t[ATTR_TILES]
            for i in range(1, TILES):
                value = jnp.where(head, chain[i - 1], chain[i])
                hi = min((i + 1) * SUB, rows)
                out[i * SUB:hi, cols] = value[: hi - i * SUB]
            return carry

        lax.fori_loop(0, n, one, 0)
        filled = filled + n

    def clear(q, carry):
        cols = pl.ds(pl.multiple_of(q * LANES, LANES), LANES)
        out[:, cols] = jnp.zeros((rows, LANES), jnp.float32)
        return carry

    lax.fori_loop(filled, slots, clear, 0)


def body(V, S, means, scales, quats, attrs, grad_screen, visible, clone_mask, rotation, shift, focal):
    G = clone_mask.shape[0]
    nblk = G // LANES
    views = grad_screen.shape[0]
    rows = means.shape[0] + scales.shape[0] + quats.shape[0] + attrs.shape[0] + 2
    T = -(-TILES // V)
    per = -(-nblk // S)
    f32, i32 = jnp.float32, jnp.int32
    mask = clone_mask.reshape(nblk, LANES)

    def lines(a):
        a = a.reshape(a.shape[:-1] + (nblk, LANES))
        return jnp.swapaxes(a, -3, -2)

    dma = pltpu.SemaphoreType.DMA
    piece = 2 * nblk // V
    peak2, meta = pl.pallas_call(
        functools.partial(stats_kernel, V, S, views),
        out_shape=(
            jax.ShapeDtypeStruct((nblk, 2, LANES), f32),
            jax.ShapeDtypeStruct((SUB, LANES), i32),
        ),
        in_specs=[spec(SMEM)] * 3 + [spec(VMEM)] * 6,
        out_specs=(spec(VMEM), spec(VMEM)),
        scratch_shapes=[
            VMEM((SUB, LANES), i32),
            VMEM((S, SUB, LANES), i32),
            VMEM((2 * nblk, LANES), f32),
            VMEM((V, piece, LANES), f32),
            VMEM((piece, LANES), f32),
            VMEM((V, piece, LANES), f32),
            VMEM((2 * nblk, LANES), f32),
            dma((S,)), dma((S,)), dma((V,)), dma((V,)), dma((V,)), dma((V,)),
        ],
        compiler_params=pltpu.CompilerParams(collective_id=0, has_side_effects=True),
        name="stats",
    )(
        rotation, shift, focal, mask, lines(means), lines(scales),
        lines(quats).reshape(-1, LANES), lines(grad_screen).reshape(views, -1, LANES),
        lines(visible).reshape(-1, LANES),
    )
    peak = jnp.swapaxes(peak2, 0, 1).reshape(2, G)
    total = meta[2, 0]
    R = T * SUB
    packed = pl.pallas_call(
        functools.partial(pack_kernel, V, S, T, per),
        out_shape=jax.ShapeDtypeStruct((S * per + 1, R, LANES), f32),
        in_specs=[spec(SMEM), spec(VMEM), spec(pl.ANY)] + [spec(VMEM)] * 4,
        out_specs=spec(VMEM),
        scratch_shapes=[
            VMEM((T, SUB, G), f32),
            VMEM((nblk, LANES), i32),
            VMEM((SUB, nblk), i32),
            SMEM((SUB, nblk), i32),
            dma((T,)), dma,
        ],
        name="pack",
    )(meta, mask, attrs, means, scales, quats, peak)
    X = V // 2
    buf = pl.pallas_call(
        functools.partial(ship_kernel, V, S, per),
        out_shape=jax.ShapeDtypeStruct((V, S * per, R, LANES), f32),
        in_specs=[spec(VMEM)],
        out_specs=spec(pl.ANY),
        scratch_shapes=[
            dma((S,)), dma((X, S)), dma((X, S)), dma((2 * X, S)), dma,
        ],
        compiler_params=pltpu.CompilerParams(collective_id=1, has_side_effects=True),
        name="ship",
    )(packed)
    clones = pl.pallas_call(
        functools.partial(place_kernel, S, T, per),
        out_shape=jax.ShapeDtypeStruct((rows, G), f32),
        in_specs=[spec(SMEM), spec(VMEM)],
        out_specs=spec(VMEM),
        compiler_params=pltpu.CompilerParams(vmem_limit_bytes=32 * 1024 * 1024),
        name="place",
    )(meta, buf)
    return peak, clones, total


def solution(mesh):
    return jax.shard_map(
        functools.partial(body, mesh.shape["view"], mesh.shape["gauss"]),
        mesh=mesh,
        in_specs=(
            P(None, "gauss"),
            P(None, "gauss"),
            P(None, "gauss"),
            P(None, "gauss"),
            P("view", None, "gauss"),
            P("view", "gauss"),
            P("gauss"),
            P("view", None, None),
            P("view", None),
            P("view"),
        ),
        out_specs=(P(None, "gauss"), P(None, "gauss"), P()),
        check_vma=False,
    )
```

profile of v0, /device:TPU:1, one launch (start us, length us, event | category | flops | bytes accessed | tf_op | source)
XLA Modules:
  0.0 119.7 jit_solution(18315341620975764058)
XLA Ops:
  0.6 1.3 %copy.16.rots = f32[4,3,3]{2,1,0:T(4,128)} copy(f32[4,3,3]{2,0,1:T(4,128)} %param.17) | data formatting | bytes 288 | tf_op args[7]
  1.9 22.9 %stats.1 = (f32[128,2,128]{2,1,0:T(2,128)}, s32[8,128]{1,0:T(8,128)}) custom-call(f32[4,3,3]{2,1,0:T(4,128)} %copy.16.rots, f32[4,3]{1,0:T(4,128)} %trns.1, f32[4]{0:T(128)} %foc.1, s32[128,128]{1,0:T(8,128)} %bitcast.32, f32[128,3,128]{2,1,0:T(4,128)} %bitcast.26, f32[128,3,128]{2,1,0:T(4,128)} %bitcast.27, f32[512,128]{1,0:T(8,128)} %bitcast.28, ...), custom_call_target="tpu_custom_call" | custom-call | tf_op jit(solution)/shard_map/stats/pallas_call | solution.py:438
  24.8 0.0 copy-start.1
  24.8 5.3 %pack.1.src = f32[129,8,128]{2,1,0:T(8,128)} custom-call(s32[8,128]{1,0:T(8,128)} %get-tuple-element.6.meta, s32[128,128]{1,0:T(8,128)} %bitcast.33, f32[49,16384]{1,0:T(8,128)} %attrs.1, f32[3,16384]{1,0:T(4,128)} %means.1, f32[3,16384]{1,0:T(4,128)} %scales.1, f32[4,16384]{1,0:T(4,128)} %quats.1, f32[2,16384]{1,0:T(2,128)} %bitcast.30), custom_call_target="tpu_custom_call" | custom-call | tf_op jit(solution)/shard_map/pack/pallas_call | solution.py:466
  30.1 82.3 %ship.1.buf = f32[8,128,8,128]{3,2,1,0:T(8,128)} custom-call(f32[129,8,128]{2,1,0:T(8,128)} %pack.1.src), custom_call_target="tpu_custom_call" | custom-call | tf_op jit(solution)/shard_map/ship/pallas_call | solution.py:481
  112.4 0.0 copy-done.1
  112.4 0.0 copy-start
  112.4 2.2 %copy-done = f32[8,128,8,128]{3,2,1,0:T(8,128)S(1)} copy-done((f32[8,128,8,128]{3,2,1,0:T(8,128)S(1)}, f32[8,128,8,128]{3,2,1,0:T(8,128)}, u32[]{:S(2)}) %copy-start) | copy-done | bytes 4194328
  114.6 0.0 copy-start.2
  114.6 4.0 %place.1 = f32[61,16384]{1,0:T(8,128)} custom-call(s32[8,128]{1,0:T(8,128)S(1)} %copy-done.1, f32[8,128,8,128]{3,2,1,0:T(8,128)S(1)} %copy-done), custom_call_target="tpu_custom_call" | custom-call | tf_op jit(solution)/shard_map/place/pallas_call | solution.py:492
  118.5 0.5 slice.3
  119.1 0.0 copy-done.2
  119.1 0.7 copy.18
Async XLA Ops:
  24.8 87.6 %copy-start.1 = (s32[8,128]{1,0:T(8,128)S(1)}, s32[8,128]{1,0:T(8,128)}, u32[]{:S(2)}) copy-start(s32[8,128]{1,0:T(8,128)} %get-tuple-element.6.meta) | copy-start | bytes 12292
  112.4 2.2 %copy-start = (f32[8,128,8,128]{3,2,1,0:T(8,128)S(1)}, f32[8,128,8,128]{3,2,1,0:T(8,128)}, u32[]{:S(2)}) copy-start(f32[8,128,8,128]{3,2,1,0:T(8,128)} %ship.1.buf) | copy-start | bytes 12582916
  114.6 4.5 %copy-start.2 = (f32[128,2,128]{2,1,0:T(2,128)S(1)}, f32[128,2,128]{2,1,0:T(2,128)}, u32[]{:S(2)}) copy-start(f32[128,2,128]{2,1,0:T(2,128)} %get-tuple-element.5) | copy-start | bytes 393220
where the time goes:
time: 120 us
  Pallas kernels  114 us (95%)
  local copies, waits for them, and re-layouts  4.65 us (4%)
    pallas_call x1, Pallas kernels, body(): pl.pallas_call(functools.partial(ship_kernel, V, S, per), out_shape=jax.S...  82.3 us
    pallas_call x1, Pallas kernels, body(): pl.pallas_call(functools.partial(stats_kernel, V, S, views), out_shape=(j...  22.9 us
    pallas_call x1, Pallas kernels, body(): pl.pallas_call(functools.partial(pack_kernel, V, S, T, per), out_shape=ja...  5.29 us
    unnamed x8, local copies, waits for them, and re-layouts  4.14 us
    pallas_call x1, Pallas kernels, body(): pl.pallas_call(functools.partial(place_kernel, S, T, per), out_shape=jax....  3.96 us

commit v1 on v0

v1 whole, which is shorter than its diff:
```python
import functools

import jax
import jax.numpy as jnp
from jax import lax
from jax.experimental import pallas as pl
from jax.experimental.pallas import tpu as pltpu
from jax.sharding import PartitionSpec as P

LANES = 128
SUB = 8
TILES = 8
VMEM = pltpu.VMEM
SMEM = pltpu.SMEM
HBM = pltpu.HBM
MESH = pl.DeviceIdType.MESH


def spec(space):
    return pl.BlockSpec(memory_space=space)


def peer(view, gauss):
    return {"view": view, "gauss": gauss}


def quat_factor(scales, quats):
    w, x, y, z = quats
    inv = 1.0 / jnp.sqrt(w * w + x * x + y * y + z * z + 0.25)
    w, x, y, z = (w * inv, x * inv, y * inv, z * inv)
    rq = [
        [1 - 2 * (y * y + z * z), 2 * (x * y - w * z), 2 * (x * z + w * y)],
        [2 * (x * y + w * z), 1 - 2 * (x * x + z * z), 2 * (y * z - w * x)],
        [2 * (x * z - w * y), 2 * (y * z + w * x), 1 - 2 * (x * x + y * y)],
    ]
    return [[rq[i][j] * scales[j] for j in range(3)] for i in range(3)]


def view_radius(means, factor, rot, trans, focal_v):
    point = [
        rot[i][0] * means[0] + rot[i][1] * means[1] + rot[i][2] * means[2] + trans[i]
        for i in range(3)
    ]
    inv = 1.0 / jnp.maximum(point[2], 1.0)
    j00 = focal_v * inv
    j02 = -(j00 * point[0]) * inv
    j12 = -(j00 * point[1]) * inv
    first = [j00 * rot[0][j] + j02 * rot[2][j] for j in range(3)]
    second = [j00 * rot[1][j] + j12 * rot[2][j] for j in range(3)]
    prow = [sum((first[j] * factor[j][k] for j in range(3))) for k in range(3)]
    qrow = [sum((second[j] * factor[j][k] for j in range(3))) for k in range(3)]
    a_val = prow[0] * prow[0] + prow[1] * prow[1] + prow[2] * prow[2] + 0.3
    c_val = qrow[0] * qrow[0] + qrow[1] * qrow[1] + qrow[2] * qrow[2] + 0.3
    b_val = prow[0] * qrow[0] + prow[1] * qrow[1] + prow[2] * qrow[2]
    half = 0.5 * (a_val - c_val)
    lam = 0.5 * (a_val + c_val) + jnp.sqrt(half * half + b_val * b_val + 0.01)
    return 3.0 * jnp.sqrt(lam)


YO = (0, 1, 3, 2)
ZO = (0, 1, 7, 2, 6, 3, 5, 4)
GROUPS = (4, 4, 8, 8, 8)


def pick(table, index):
    out = jnp.full(index.shape, table[0], jnp.int32)
    for i in range(1, len(table)):
        out = jnp.where(index == i, table[i], out)
    return out


def main_kernel(
    V, S, views, rots_h, trns_h, foc_h, mask_h, means_h, scales_h, quats_h, attrs_h, grad_h, vis_h,
    buf, peak, where_out,
    rots, trns, foc, mask, means, scales, quats, grad, vis, x, enc, g, split, send, cnt, counts,
    local, halves, merged, whole, lsem, csend, crecv, rsend, rrecv, asend, arecv,
    fsend, frecv, xsend, xrecv, hsend, hrecv, msend, mrecv,
):
    v, s = lax.axis_index("view"), lax.axis_index("gauss")
    nblk = mask.shape[0]
    per = nblk // S
    Z = len(ZO)
    Y = len(YO)
    X = V // 2
    core = lax.rem(v, 2)
    chip = lax.div(v, 2)
    mate = v + 1 - 2 * core
    nxt = 2 * lax.rem(chip + 1, X) + core
    prv = 2 * lax.rem(chip + X - 1, X) + core
    opp = 2 * lax.rem(chip + 2, X) + core
    y, z = lax.div(s, Z), lax.rem(s, Z)
    i32, f32, bf16 = jnp.int32, jnp.float32, jnp.bfloat16

    def dest(p):
        return lax.rem(y + YO[p // Z], Y) * Z + lax.rem(z + ZO[p % Z], Z)

    bar = pltpu.get_barrier_semaphore()
    for p in range(1, S):
        pl.semaphore_signal(bar, inc=1, device_id=peer(v, dest(p)), device_id_type=MESH)
    for k in range(1, V):
        pl.semaphore_signal(bar, inc=1, device_id=peer(lax.rem(v + k, V), s), device_id_type=MESH)

    loads = [
        pltpu.make_async_copy(a, b, lsem.at[i])
        for i, (a, b) in enumerate((
            (mask_h, mask), (means_h, means), (scales_h, scales), (quats_h, quats),
            (grad_h, grad), (vis_h, vis), (rots_h, rots), (trns_h, trns), (foc_h, foc),
        ))
    ]
    for c in loads:
        c.start()

    def tiles(act):
        for t in range(1, TILES):
            @pl.when(v == t)
            def _():
                n = 6 if t < TILES - 1 else 1
                act(pltpu.make_async_copy(
                    attrs_h.at[pl.ds((t - 1) * SUB, n), :], x.at[pl.ds(0, n), :], lsem.at[9]
                ))
                if t > 1:
                    act(pltpu.make_async_copy(
                        attrs_h.at[pl.ds((t - 2) * SUB + 6, 2), :], x.at[pl.ds(6, 2), :], lsem.at[10]
                    ))

    tiles(lambda c: c.start())

    loads[0].wait()
    m = mask[...]
    cnt[...] = jnp.full((1, LANES), jnp.sum(m), i32)
    lane = lax.broadcasted_iota(i32, (nblk, LANES), 1)
    row = lax.broadcasted_iota(i32, (nblk, LANES), 0)
    mb = m.astype(bf16)
    before = (row < lane).astype(bf16)
    above = (row > lane).astype(bf16)
    dot = functools.partial(jnp.dot, preferred_element_type=f32)
    ones = jnp.ones((LANES, LANES), bf16)
    rank = dot(mb, before).astype(i32)
    size = dot(mb, ones).astype(i32)
    base = dot(dot(above, mb).astype(bf16), ones).astype(i32)
    flat = lax.dot_general(
        jnp.ones((SUB, LANES), bf16), mb, (((1,), (1,)), ((), ())), preferred_element_type=f32
    )
    starts = dot(flat.astype(bf16), before).astype(i32)
    code = jnp.where(m == 1, 65536 + (lane - rank) * 256 + lane, 0)
    bit = 1
    while bit < LANES:
        moved = pltpu.roll(code, LANES - bit, 1)
        goes = (moved & (bit * 256)) != 0
        stays = (code & (bit * 256)) == 0
        code = jnp.where(goes, moved, jnp.where(stays, code, 0))
        bit *= 2
    turn = (lane - base) & (LANES - 1)
    src = jnp.take_along_axis(code & (LANES - 1), turn, axis=1)
    valid = turn < size
    idx = jnp.where(valid, src, 0)
    enc[...] = jnp.where(valid, src, -1)
    head = lane >= (base & (LANES - 1))
    low, high = valid & head, valid & jnp.logical_not(head)

    for c in loads[1:]:
        c.wait()
    step = 2 * SUB

    def chunk(i, carry):
        rows = pl.ds(pl.multiple_of(i * step, step), step)

        def lines(ref, count, c):
            return ref[pl.ds(i * step * count + c, step, stride=count), :]

        mm = [means[rows, c, :] for c in range(3)]
        factor = quat_factor(
            [scales[rows, c, :] for c in range(3)], [lines(quats, 4, c) for c in range(4)]
        )
        gmax = jnp.zeros((step, LANES), f32)
        rmax = jnp.zeros((step, LANES), f32)
        for u in range(views):
            rot = [[rots[a, u, b] for b in range(3)] for a in range(3)]
            trans = [trns[u, a] for a in range(3)]
            radius = view_radius(mm, factor, rot, trans, foc[u])
            seen = lines(vis, views, u).astype(f32)
            g0, g1 = (grad[u, pl.ds(i * step * 2 + c, step, stride=2), :] for c in range(2))
            gmax = jnp.maximum(gmax, jnp.sqrt(g0 * g0 + g1 * g1) * seen)
            rmax = jnp.maximum(rmax, radius * seen)
        local[pl.ds(i * step * 2, step, stride=2), :] = gmax
        local[pl.ds(i * step * 2 + 1, step, stride=2), :] = rmax
        return carry

    lax.fori_loop(0, nblk // step, chunk, 0)

    started = []

    def remote(a, b, ss, rs, to):
        return pltpu.make_async_remote_copy(
            src_ref=a, dst_ref=b, send_sem=ss, recv_sem=rs, device_id=to, device_id_type=MESH
        )

    def go(copy):
        copy.start()
        started.append(copy)
        return copy

    pl.semaphore_wait(bar, S + V - 2)
    tally = [
        go(remote(cnt, counts.at[pl.ds(p, 1), :], csend.at[p], crecv.at[p], peer(v, dest(p))))
        for p in range(1, S)
    ]
    piece = 2 * nblk // V
    scatter = []
    for k in range(1, V):
        to = lax.rem(v + k, V)
        part = local.at[pl.ds(pl.multiple_of(to * piece, piece), piece), :]
        scatter.append(go(remote(part, halves.at[k], rsend.at[k], rrecv.at[k], peer(to, s))))
    counts[0:1, :] = cnt[...]

    tiles(lambda c: c.wait())

    @pl.when(v > 0)
    def _():
        def gather(b, carry):
            e = jnp.broadcast_to(enc[pl.ds(b, 1), :], (SUB, LANES))
            cols = pl.ds(pl.multiple_of(b * LANES, LANES), LANES)
            got = jnp.take_along_axis(x[:, cols], jnp.maximum(e, 0), axis=1)
            g[b] = got
            return carry

        lax.fori_loop(0, nblk, gather, 0, unroll=8)

    def put(final, value):
        g[:, (final + 6) % SUB, :] = jnp.take_along_axis(value, idx, axis=1)

    @pl.when(v == 0)
    def _():
        for c in range(3):
            put(c, means[:, c, :])
            put(3 + c, scales[:, c, :])
        for c in range(2):
            put(6 + c, quats[pl.ds(c, nblk, stride=4), :])

    @pl.when(v == 1)
    def _():
        for c in range(2):
            put(c, quats[pl.ds(2 + c, nblk, stride=4), :])

    def cut(c):
        value = g[:, (c + 6) % SUB, :]
        for part, keep in enumerate((low, high)):
            rest = jnp.where(keep, value, 0.0)
            for i in range(3):
                top = rest.astype(bf16)
                split[(2 * i + part) * nblk:(2 * i + part + 1) * nblk, c * LANES:(c + 1) * LANES] = top
                rest = rest - top.astype(f32)

    for c in range(3):
        cut(c)

    @pl.when(v < TILES - 1)
    def _():
        for c in range(3, SUB):
            cut(c)

    for c in scatter:
        c.wait_recv()
    mine = pl.ds(pl.multiple_of(v * piece, piece), piece)
    best = local[mine, :]
    for k in range(1, V):
        best = jnp.maximum(best, halves[k])
    merged[...] = best
    spread = [
        go(remote(merged, whole.at[k], asend.at[k], arecv.at[k], peer(lax.rem(v + k, V), s)))
        for k in range(1, V)
    ]
    peak[mine, :] = best
    for k in range(1, V):
        spread[k - 1].wait_recv()
        who = lax.rem(v + V - k, V)
        peak[pl.ds(pl.multiple_of(who * piece, piece), piece), :] = whole[k]

    @pl.when(v == TILES - 1)
    def _():
        for c in range(2):
            put(3 + c, peak[pl.ds(c, nblk, stride=2), :])
        for c in range(5, SUB):
            g[:, (c + 6) % SUB, :] = jnp.zeros((nblk, LANES), f32)
        for c in range(3, SUB):
            cut(c)

    for c in tally:
        c.wait_recv()
    tot = counts[...]
    blocks = (tot + (LANES - 1)) >> 7

    def source(p):
        return ((y - pick(YO, p >> 3)) & (Y - 1)) * Z + ((z - pick(ZO, p & 7)) & (Z - 1))

    pr = lax.broadcasted_iota(i32, (S, S), 0)
    pc = lax.broadcasted_iota(i32, (S, S), 1)
    less = (source(pc) < source(pr)).astype(bf16)
    offs = dot(less, blocks.astype(bf16)).astype(i32)
    t = ((y + pick(YO, row >> 5)) & (Y - 1)) * Z + ((z + pick(ZO, (row >> 2) & 7)) & (Z - 1))
    d = ((t - offs[0:1, :]) & (S - 1)) + ((row & (per - 1)) << 5)
    at = starts[0:1, :] >> 7
    a_low = (d == at).astype(bf16)
    a_high = (d == at + 1).astype(bf16)
    hot = jnp.concatenate([a_low, a_high] * 3, axis=1)
    moved = dot(hot, split[...])
    for c in range(SUB):
        send[:, c, :] = moved[:, c * LANES:(c + 1) * LANES]

    k = lax.broadcasted_iota(i32, (S, LANES), 1) * S + s
    p32 = lax.broadcasted_iota(i32, (S, LANES), 0)
    here = (k >= offs) & (k < offs + blocks)
    spot = jnp.where(here, p32 * per + ((k - offs) >> 5) + 1, 0)
    found = jnp.sum(spot, axis=0, keepdims=True) - 1
    total = jnp.sum(tot, axis=0, keepdims=True)
    sub = lax.broadcasted_iota(i32, (SUB, LANES), 0)
    where_out[...] = jnp.where(sub == 0, found, total)

    fars = [None]
    for p in range(1, S):
        fars.append(go(remote(
            send.at[pl.ds(p * per, per)], buf.at[v, pl.ds(p * per, per)],
            fsend.at[p], frecv.at[p], peer(v, dest(p)),
        )))
    own = pltpu.make_async_copy(send.at[pl.ds(0, per)], buf.at[v, pl.ds(0, per)], fsend.at[0])
    own.start()

    edges = [0]
    for n in GROUPS:
        edges.append(edges[-1] + n)
    N = len(GROUPS)

    def group(owner, i, half=None):
        first, size = edges[i] * per, GROUPS[i] * per
        if half is not None:
            size //= 2
            first += half * size
        return buf.at[owner, pl.ds(first, size)]

    def ring(i, way):
        return remote(group(v, i), group(v, i), xsend.at[way, i], xrecv.at[way, i], peer((nxt, prv)[way], s))

    def relay(i, way):
        ref = group((prv, nxt)[way], i, way)
        return remote(ref, ref, hsend.at[way, i], hrecv.at[way, i], peer((nxt, prv)[way], s))

    def beside(i, q):
        ref = group((v, prv, nxt, opp)[q], i)
        return remote(ref, ref, msend.at[q, i], mrecv.at[q, i], peer(mate, s))

    rings, relays, besides = {}, {}, {}
    for i in range(N + 2):
        if i < N:
            for p in range(edges[i], edges[i + 1]):
                if p:
                    fars[p].wait_recv()
                else:
                    own.wait()
            for way in range(2):
                rings[i, way] = go(ring(i, way))
            besides[i, 0] = go(beside(i, 0))
        if 1 <= i <= N:
            for way in range(2):
                rings[i - 1, way].wait_recv()
                relays[i - 1, way] = go(relay(i - 1, way))
                besides[i - 1, 1 + way] = go(beside(i - 1, 1 + way))
        if i >= 2:
            for way in range(2):
                relays[i - 2, way].wait_recv()
            besides[i - 2, 3] = go(beside(i - 2, 3))
    for c in besides.values():
        c.wait_recv()
    for c in started:
        c.wait_send()


def place_kernel(idx_v, peak_in, buf, clones, peak, total, out, idx, isem, osem, psem):
    rows = clones.shape[0]
    slots = out.shape[1] // LANES
    chunks = osem.shape[0]
    fetch = pltpu.make_async_copy(idx_v, idx, isem)
    fetch.start()
    top = pltpu.make_async_copy(peak_in, peak, psem)
    top.start()
    fetch.wait()
    total[0] = idx[1, 0]
    each = slots // chunks
    outs = []
    for c in range(chunks):
        def one(q, carry):
            r = idx[0, q]
            on = r >= 0
            r = jnp.maximum(r, 0)
            cols = pl.ds(pl.multiple_of(q * LANES, LANES), LANES)
            for i in range(TILES):
                n = min(rows - i * SUB, SUB)
                out[i * SUB:i * SUB + n, cols] = jnp.where(on, buf[i, r], 0.0)[:n]
            return carry

        lax.fori_loop(c * each, (c + 1) * each, one, 0, unroll=4)
        cols = pl.ds(c * each * LANES, each * LANES)
        cp = pltpu.make_async_copy(out.at[:, cols], clones.at[:, cols], osem.at[c])
        cp.start()
        outs.append(cp)
    for cp in outs:
        cp.wait()
    top.wait()


def body(V, S, means, scales, quats, attrs, grad_screen, visible, clone_mask, rotation, shift, focal):
    G = clone_mask.shape[0]
    nblk = G // LANES
    views = grad_screen.shape[0]
    rows = means.shape[0] + scales.shape[0] + quats.shape[0] + attrs.shape[0] + 2
    f32, i32 = jnp.float32, jnp.int32

    def lines(a):
        a = a.reshape(a.shape[:-1] + (nblk, LANES))
        return jnp.swapaxes(a, -3, -2)

    dma = pltpu.SemaphoreType.DMA
    piece = 2 * nblk // V
    N = len(GROUPS)
    limit = 32 * 1024 * 1024
    buf, peak, where = pl.pallas_call(
        functools.partial(main_kernel, V, S, views),
        out_shape=(
            VMEM((V, nblk, SUB, LANES), f32), VMEM((2 * nblk, LANES), f32), VMEM((SUB, LANES), i32),
        ),
        in_specs=[spec(HBM)] * 10,
        out_specs=(spec(VMEM),) * 3,
        scratch_shapes=[
            SMEM((3, views, 3), f32),
            SMEM((views, 3), f32),
            SMEM((views,), f32),
            VMEM((nblk, LANES), i32),
            VMEM((nblk, 3, LANES), f32),
            VMEM((nblk, 3, LANES), f32),
            VMEM((4 * nblk, LANES), f32),
            VMEM((views, 2 * nblk, LANES), f32),
            VMEM((views * nblk, LANES), i32),
            VMEM((SUB, G), f32),
            VMEM((nblk, LANES), i32),
            VMEM((nblk, SUB, LANES), f32),
            VMEM((6 * nblk, SUB * LANES), jnp.bfloat16),
            VMEM((nblk, SUB, LANES), f32),
            VMEM((1, LANES), i32),
            VMEM((S, LANES), i32),
            VMEM((2 * nblk, LANES), f32),
            VMEM((V, piece, LANES), f32),
            VMEM((piece, LANES), f32),
            VMEM((V, piece, LANES), f32),
            dma((11,)), dma((S,)), dma((S,)), dma((V,)), dma((V,)), dma((V,)), dma((V,)),
            dma((S,)), dma((S,)), dma((2, N)), dma((2, N)), dma((2, N)), dma((2, N)),
            dma((4, N)), dma((4, N)),
        ],
        compiler_params=pltpu.CompilerParams(
            collective_id=0, has_side_effects=True, vmem_limit_bytes=limit
        ),
        name="main",
    )(*(
        pltpu.with_memory_space_constraint(a, HBM)
        for a in (
            jnp.transpose(rotation, (1, 0, 2)), shift, focal, clone_mask.reshape(nblk, LANES),
            lines(means), lines(scales), lines(quats).reshape(-1, LANES), attrs,
            lines(grad_screen).reshape(views, -1, LANES), lines(visible).reshape(-1, LANES),
        )
    ))
    chunks = 8
    clones, peak, total = pl.pallas_call(
        place_kernel,
        out_shape=(
            jax.ShapeDtypeStruct((rows, G), f32),
            jax.ShapeDtypeStruct((2 * nblk, LANES), f32),
            jax.ShapeDtypeStruct((1,), i32),
        ),
        in_specs=[spec(VMEM)] * 3,
        out_specs=(spec(pl.ANY), spec(pl.ANY), spec(SMEM)),
        scratch_shapes=[VMEM((rows, G), f32), SMEM((SUB, LANES), i32), dma, dma((chunks,)), dma],
        compiler_params=pltpu.CompilerParams(vmem_limit_bytes=limit),
        name="place",
    )(where, peak, buf)
    peak = jnp.swapaxes(peak.reshape(nblk, 2, LANES), 0, 1).reshape(2, G)
    return peak, clones, total.reshape(())


def solution(mesh):
    return jax.shard_map(
        functools.partial(body, mesh.shape["view"], mesh.shape["gauss"]),
        mesh=mesh,
        in_specs=(
            P(None, "gauss"),
            P(None, "gauss"),
            P(None, "gauss"),
            P(None, "gauss"),
            P("view", None, "gauss"),
            P("view", "gauss"),
            P("gauss"),
            P("view", None, None),
            P("view", None),
            P("view"),
        ),
        out_specs=(P(None, "gauss"), P(None, "gauss"), P()),
        check_vma=False,
    )
```

time: 120 us -> 58.7 us (0.49)
  Pallas kernels: 114 us -> 58 us
  local copies, waits for them, and re-layouts: 4.65 us -> 0 us
    pallas_call x4 -> x2, Pallas kernels: 114 us -> 58 us  [the longest x1 54.6 us: body(): pl.pallas_call(functools.partial(main_kernel, V, S, views), out_shape=(VM...]
    unnamed x8 -> x0, local copies, waits for them, and re-layouts: 4.14 us -> none
where the time goes in v1:
time: 58.7 us; the launch traced here: 58.6 us
  Pallas kernels  58 us (99%)
  between operations  0.64 us (1%)
    pallas_call x1, Pallas kernels, body(): pl.pallas_call(functools.partial(main_kernel, V, S, views), out_shape=(VM...  54.6 us
    pallas_call x1, Pallas kernels, body(): pl.pallas_call(place_kernel, out_shape=(jax.ShapeDtypeStruct((rows, G), f...  3.32 us

profile of v1, /device:TPU:1, one launch (start us, length us, event | category | flops | bytes accessed | tf_op | source)
XLA Modules:
  0.0 58.6 jit_solution(1141456400553739523)
XLA Ops:
  0.6 54.6 %main.1 = (f32[8,128,8,128]{3,2,1,0:T(8,128)S(1)}, f32[256,128]{1,0:T(8,128)S(1)}, s32[8,128]{1,0:T(8,128)S(1)}) custom-call(f32[3,4,3]{2,1,0:T(4,128)} %bitcast.35, f32[4,3]{1,0:T(4,128)} %trns_h.1, f32[4]{0:T(128)} %foc_h.1, s32[128,128]{1,0:T(8,128)} %bitcast.34, f32[128,3,128]{2,1,0:T(4,128)} %bitcast.30, f32[128,3,128]{2,1,0:T(4,128)} %bitcast.31, ...), custom_call_target="tpu_custom_call" | custom-call | tf_op jit(solution)/shard_map/main/pallas_call | solution.py:425
  55.3 3.3 %place.1 = (f32[61,16384]{1,0:T(8,128)}, f32[256,128]{1,0:T(8,128)}, s32[1]{0:T(128)}) custom-call(s32[8,128]{1,0:T(8,128)S(1)} %get-tuple-element.9.idx_v, f32[256,128]{1,0:T(8,128)S(1)} %get-tuple-element.10.peak_in, f32[8,128,8,128]{3,2,1,0:T(8,128)S(1)} %get-tuple-element.11.buf), custom_call_target="tpu_custom_call" | custom-call | tf_op jit(solution)/shard_map/place/pallas_call | solution.py:470

commit v2 on v1

--- a/solution.py
+++ b/solution.py
@@ -26,7 +26,7 @@
 
 def quat_factor(scales, quats):
     w, x, y, z = quats
-    inv = 1.0 / jnp.sqrt(w * w + x * x + y * y + z * z + 0.25)
+    inv = lax.rsqrt(w * w + x * x + y * y + z * z + 0.25)
     w, x, y, z = (w * inv, x * inv, y * inv, z * inv)
     rq = [
         [1 - 2 * (y * y + z * z), 2 * (x * y - w * z), 2 * (x * z + w * y)],
@@ -36,7 +36,7 @@
     return [[rq[i][j] * scales[j] for j in range(3)] for i in range(3)]
 
 
-def view_radius(means, factor, rot, trans, focal_v):
+def view_lam(means, factor, rot, trans, focal_v):
     point = [
         rot[i][0] * means[0] + rot[i][1] * means[1] + rot[i][2] * means[2] + trans[i]
         for i in range(3)
@@ -53,13 +53,13 @@
     c_val = qrow[0] * qrow[0] + qrow[1] * qrow[1] + qrow[2] * qrow[2] + 0.3
     b_val = prow[0] * qrow[0] + prow[1] * qrow[1] + prow[2] * qrow[2]
     half = 0.5 * (a_val - c_val)
-    lam = 0.5 * (a_val + c_val) + jnp.sqrt(half * half + b_val * b_val + 0.01)
-    return 3.0 * jnp.sqrt(lam)
+    disc = half * half + b_val * b_val + 0.01
+    return 0.5 * (a_val + c_val) + disc * lax.rsqrt(disc)
 
 
 YO = (0, 1, 3, 2)
 ZO = (0, 1, 7, 2, 6, 3, 5, 4)
-GROUPS = (4, 4, 8, 8, 8)
+GROUPS = (2, 2, 4, 8, 8, 8)
 
 
 def pick(table, index):
@@ -72,8 +72,8 @@
 def main_kernel(
     V, S, views, rots_h, trns_h, foc_h, mask_h, means_h, scales_h, quats_h, attrs_h, grad_h, vis_h,
     buf, peak, where_out,
-    rots, trns, foc, mask, means, scales, quats, grad, vis, x, enc, g, split, send, cnt, counts,
-    local, halves, merged, whole, lsem, csend, crecv, rsend, rrecv, asend, arecv,
+    rots, trns, foc, mask, means, scales, quats, grad, vis, fac, x, enc, g, split, packed, send, cnt, counts,
+    local, halves, merged, whole, lsem, csend, crecv, psend, precv,
     fsend, frecv, xsend, xrecv, hsend, hrecv, msend, mrecv,
 ):
     v, s = lax.axis_index("view"), lax.axis_index("gauss")
@@ -97,8 +97,8 @@
     bar = pltpu.get_barrier_semaphore()
     for p in range(1, S):
         pl.semaphore_signal(bar, inc=1, device_id=peer(v, dest(p)), device_id_type=MESH)
-    for k in range(1, V):
-        pl.semaphore_signal(bar, inc=1, device_id=peer(lax.rem(v + k, V), s), device_id_type=MESH)
+    for to in (mate, nxt, prv, opp):
+        pl.semaphore_signal(bar, inc=1, device_id=peer(to, s), device_id_type=MESH)
 
     loads = [
         pltpu.make_async_copy(a, b, lsem.at[i])
@@ -123,11 +123,73 @@
                         attrs_h.at[pl.ds((t - 2) * SUB + 6, 2), :], x.at[pl.ds(6, 2), :], lsem.at[10]
                     ))
 
-    tiles(lambda c: c.start())
-
     loads[0].wait()
     m = mask[...]
     cnt[...] = jnp.full((1, LANES), jnp.sum(m), i32)
+    step = 2 * SUB
+
+    def lines(ref, i, count, c):
+        return ref[pl.ds(i * step * count + c, step, stride=count), :]
+
+    for i in (1, 2, 3):
+        loads[i].wait()
+
+    def shape(i, carry):
+        rows = pl.ds(pl.multiple_of(i * step, step), step)
+        factor = quat_factor(
+            [scales[rows, c, :] for c in range(3)], [lines(quats, i, 4, c) for c in range(4)]
+        )
+        for c in range(3):
+            fac[9 + c, rows, :] = means[rows, c, :]
+            for e in range(3):
+                fac[3 * c + e, rows, :] = factor[c][e]
+        return carry
+
+    lax.fori_loop(0, nblk // step, shape, 0)
+    for i in range(4, 9):
+        loads[i].wait()
+    tiles(lambda c: c.start())
+    for u in range(views):
+        rot = [[rots[a, u, b] for b in range(3)] for a in range(3)]
+        trans = [trns[u, a] for a in range(3)]
+        fl = foc[u]
+
+        def look(i, carry):
+            rows = pl.ds(pl.multiple_of(i * step, step), step)
+            factor = [[fac[3 * a + b, rows, :] for b in range(3)] for a in range(3)]
+            lam = view_lam([fac[9 + c, rows, :] for c in range(3)], factor, rot, trans, fl)
+            seen = lines(vis, i, views, u) != 0
+            g0, g1 = (grad[u, pl.ds(i * step * 2 + c, step, stride=2), :] for c in range(2))
+            for c, value in enumerate((g0 * g0 + g1 * g1, lam)):
+                at = pl.ds(i * step * 2 + c, step, stride=2)
+                value = jnp.where(seen, value, 0.0)
+                local[at, :] = value if u == 0 else jnp.maximum(local[at, :], value)
+            return carry
+
+        lax.fori_loop(0, nblk // step, look, 0)
+
+    started = []
+
+    def remote(a, b, ss, rs, to):
+        return pltpu.make_async_remote_copy(
+            src_ref=a, dst_ref=b, send_sem=ss, recv_sem=rs, device_id=to, device_id_type=MESH
+        )
+
+    def go(copy):
+        copy.start()
+        started.append(copy)
+        return copy
+
+    pl.semaphore_wait(bar, S + 3)
+    tally = [
+        go(remote(cnt, counts.at[pl.ds(p, 1), :], csend.at[p], crecv.at[p], peer(v, dest(p))))
+        for p in range(1, S)
+    ]
+    mine = pl.ds(pl.multiple_of(core * nblk, nblk), nblk)
+    other = pl.ds(pl.multiple_of((1 - core) * nblk, nblk), nblk)
+    pair = go(remote(local.at[other, :], halves, psend.at[0], precv.at[0], peer(mate, s)))
+    counts[0:1, :] = cnt[...]
+
     lane = lax.broadcasted_iota(i32, (nblk, LANES), 1)
     row = lax.broadcasted_iota(i32, (nblk, LANES), 0)
     mb = m.astype(bf16)
@@ -158,60 +220,13 @@
     head = lane >= (base & (LANES - 1))
     low, high = valid & head, valid & jnp.logical_not(head)
 
-    for c in loads[1:]:
-        c.wait()
-    step = 2 * SUB
-
-    def chunk(i, carry):
-        rows = pl.ds(pl.multiple_of(i * step, step), step)
-
-        def lines(ref, count, c):
-            return ref[pl.ds(i * step * count + c, step, stride=count), :]
-
-        mm = [means[rows, c, :] for c in range(3)]
-        factor = quat_factor(
-            [scales[rows, c, :] for c in range(3)], [lines(quats, 4, c) for c in range(4)]
-        )
-        gmax = jnp.zeros((step, LANES), f32)
-        rmax = jnp.zeros((step, LANES), f32)
-        for u in range(views):
-            rot = [[rots[a, u, b] for b in range(3)] for a in range(3)]
-            trans = [trns[u, a] for a in range(3)]
-            radius = view_radius(mm, factor, rot, trans, foc[u])
-            seen = lines(vis, views, u).astype(f32)
-            g0, g1 = (grad[u, pl.ds(i * step * 2 + c, step, stride=2), :] for c in range(2))
-            gmax = jnp.maximum(gmax, jnp.sqrt(g0 * g0 + g1 * g1) * seen)
-            rmax = jnp.maximum(rmax, radius * seen)
-        local[pl.ds(i * step * 2, step, stride=2), :] = gmax
-        local[pl.ds(i * step * 2 + 1, step, stride=2), :] = rmax
-        return carry
-
-    lax.fori_loop(0, nblk // step, chunk, 0)
-
-    started = []
-
-    def remote(a, b, ss, rs, to):
-        return pltpu.make_async_remote_copy(
-            src_ref=a, dst_ref=b, send_sem=ss, recv_sem=rs, device_id=to, device_id_type=MESH
-        )
-
-    def go(copy):
-        copy.start()
-        started.append(copy)
-        return copy
-
-    pl.semaphore_wait(bar, S + V - 2)
-    tally = [
-        go(remote(cnt, counts.at[pl.ds(p, 1), :], csend.at[p], crecv.at[p], peer(v, dest(p))))
-        for p in range(1, S)
+
+    pair.wait_recv()
+    merged[...] = jnp.maximum(local[mine, :], halves[...])
+    spread = [
+        go(remote(merged, whole.at[k], psend.at[1 + k], precv.at[1 + k], peer(to, s)))
+        for k, to in enumerate((nxt, prv, opp))
     ]
-    piece = 2 * nblk // V
-    scatter = []
-    for k in range(1, V):
-        to = lax.rem(v + k, V)
-        part = local.at[pl.ds(pl.multiple_of(to * piece, piece), piece), :]
-        scatter.append(go(remote(part, halves.at[k], rsend.at[k], rrecv.at[k], peer(to, s))))
-    counts[0:1, :] = cnt[...]
 
     tiles(lambda c: c.wait())
 
@@ -251,70 +266,58 @@
                 split[(2 * i + part) * nblk:(2 * i + part + 1) * nblk, c * LANES:(c + 1) * LANES] = top
                 rest = rest - top.astype(f32)
 
-    for c in range(3):
-        cut(c)
+    at = starts[0:1, :] >> 7
+    hot = jnp.concatenate([(row == at).astype(bf16), (row == at + 1).astype(bf16)] * 3, axis=1)
+
+    def pack(*finals):
+        for c in finals:
+            cut(c)
+        lo, hi = finals[0], finals[-1] + 1
+        moved = dot(hot, split[:, lo * LANES:hi * LANES])
+        for c in finals:
+            packed[:, c, :] = moved[:, (c - lo) * LANES:(c - lo + 1) * LANES]
+
+    full = remote(peak.at[mine, :], peak.at[mine, :], psend.at[4], precv.at[4], peer(mate, s))
+
+    def finish():
+        for c in spread:
+            c.wait_recv()
+        best = merged[...]
+        for k in range(3):
+            best = jnp.maximum(best, whole[k])
+        odd = (lax.broadcasted_iota(i32, best.shape, 0) & 1) == 1
+        peak[mine, :] = jnp.sqrt(best) * jnp.where(odd, 3.0, 1.0)
+        full.start()
+        full.wait_recv()
+
+    pack(0, 1, 2)
 
     @pl.when(v < TILES - 1)
     def _():
-        for c in range(3, SUB):
-            cut(c)
-
-    for c in scatter:
-        c.wait_recv()
-    mine = pl.ds(pl.multiple_of(v * piece, piece), piece)
-    best = local[mine, :]
-    for k in range(1, V):
-        best = jnp.maximum(best, halves[k])
-    merged[...] = best
-    spread = [
-        go(remote(merged, whole.at[k], asend.at[k], arecv.at[k], peer(lax.rem(v + k, V), s)))
-        for k in range(1, V)
-    ]
-    peak[mine, :] = best
-    for k in range(1, V):
-        spread[k - 1].wait_recv()
-        who = lax.rem(v + V - k, V)
-        peak[pl.ds(pl.multiple_of(who * piece, piece), piece), :] = whole[k]
+        pack(3, 4, 5, 6, 7)
 
     @pl.when(v == TILES - 1)
     def _():
+        packed[:, 5:, :] = jnp.zeros((nblk, 3, LANES), f32)
+        finish()
         for c in range(2):
             put(3 + c, peak[pl.ds(c, nblk, stride=2), :])
-        for c in range(5, SUB):
-            g[:, (c + 6) % SUB, :] = jnp.zeros((nblk, LANES), f32)
-        for c in range(3, SUB):
-            cut(c)
-
+        pack(3, 4)
+
+    def source(p):
+        return ((y - pick(YO, p >> 3)) & (Y - 1)) * Z + ((z - pick(ZO, p & 7)) & (Z - 1))
+
+    p32 = lax.broadcasted_iota(i32, (S, LANES), 0)
+    lower = source(p32) < s
     for c in tally:
         c.wait_recv()
     tot = counts[...]
     blocks = (tot + (LANES - 1)) >> 7
-
-    def source(p):
-        return ((y - pick(YO, p >> 3)) & (Y - 1)) * Z + ((z - pick(ZO, p & 7)) & (Z - 1))
-
-    pr = lax.broadcasted_iota(i32, (S, S), 0)
-    pc = lax.broadcasted_iota(i32, (S, S), 1)
-    less = (source(pc) < source(pr)).astype(bf16)
-    offs = dot(less, blocks.astype(bf16)).astype(i32)
-    t = ((y + pick(YO, row >> 5)) & (Y - 1)) * Z + ((z + pick(ZO, (row >> 2) & 7)) & (Z - 1))
-    d = ((t - offs[0:1, :]) & (S - 1)) + ((row & (per - 1)) << 5)
-    at = starts[0:1, :] >> 7
-    a_low = (d == at).astype(bf16)
-    a_high = (d == at + 1).astype(bf16)
-    hot = jnp.concatenate([a_low, a_high] * 3, axis=1)
-    moved = dot(hot, split[...])
-    for c in range(SUB):
-        send[:, c, :] = moved[:, c * LANES:(c + 1) * LANES]
-
-    k = lax.broadcasted_iota(i32, (S, LANES), 1) * S + s
-    p32 = lax.broadcasted_iota(i32, (S, LANES), 0)
-    here = (k >= offs) & (k < offs + blocks)
-    spot = jnp.where(here, p32 * per + ((k - offs) >> 5) + 1, 0)
-    found = jnp.sum(spot, axis=0, keepdims=True) - 1
-    total = jnp.sum(tot, axis=0, keepdims=True)
-    sub = lax.broadcasted_iota(i32, (SUB, LANES), 0)
-    where_out[...] = jnp.where(sub == 0, found, total)
+    offset = jnp.sum(jnp.where(lower, blocks, 0), axis=0)[0]
+    for p in range(S):
+        first = (dest(p) - offset) & (S - 1)
+        for w in range(per):
+            send[p * per + w] = packed[first + S * w]
 
     fars = [None]
     for p in range(1, S):
@@ -324,6 +327,23 @@
         )))
     own = pltpu.make_async_copy(send.at[pl.ds(0, per)], buf.at[v, pl.ds(0, per)], fsend.at[0])
     own.start()
+
+    @pl.when(v < TILES - 1)
+    def _():
+        finish()
+
+    started.append(full)
+    pr = lax.broadcasted_iota(i32, (S, S), 0)
+    pc = lax.broadcasted_iota(i32, (S, S), 1)
+    less = (source(pc) < source(pr)).astype(bf16)
+    offs = dot(less, blocks.astype(bf16)).astype(i32)
+    k = lax.broadcasted_iota(i32, (S, LANES), 1) * S + s
+    here = (k >= offs) & (k < offs + blocks)
+    spot = jnp.where(here, p32 * per + ((k - offs) >> 5) + 1, 0)
+    found = jnp.sum(spot, axis=0, keepdims=True) - 1
+    total = jnp.sum(tot, axis=0, keepdims=True)
+    sub = lax.broadcasted_iota(i32, (SUB, LANES), 0)
+    where_out[...] = jnp.where(sub == 0, found, total)
 
     edges = [0]
     for n in GROUPS:
@@ -419,7 +439,6 @@
         return jnp.swapaxes(a, -3, -2)
 
     dma = pltpu.SemaphoreType.DMA
-    piece = 2 * nblk // V
     N = len(GROUPS)
     limit = 32 * 1024 * 1024
     buf, peak, where = pl.pallas_call(
@@ -439,18 +458,20 @@
             VMEM((4 * nblk, LANES), f32),
             VMEM((views, 2 * nblk, LANES), f32),
             VMEM((views * nblk, LANES), i32),
+            VMEM((12, nblk, LANES), f32),
             VMEM((SUB, G), f32),
             VMEM((nblk, LANES), i32),
             VMEM((nblk, SUB, LANES), f32),
             VMEM((6 * nblk, SUB * LANES), jnp.bfloat16),
             VMEM((nblk, SUB, LANES), f32),
+            VMEM((nblk, SUB, LANES), f32),
             VMEM((1, LANES), i32),
             VMEM((S, LANES), i32),
             VMEM((2 * nblk, LANES), f32),
-            VMEM((V, piece, LANES), f32),
-            VMEM((piece, LANES), f32),
-            VMEM((V, piece, LANES), f32),
-            dma((11,)), dma((S,)), dma((S,)), dma((V,)), dma((V,)), dma((V,)), dma((V,)),
+            VMEM((nblk, LANES), f32),
+            VMEM((nblk, LANES), f32),
+            VMEM((3, nblk, LANES), f32),
+            dma((11,)), dma((S,)), dma((S,)), dma((5,)), dma((5,)),
             dma((S,)), dma((S,)), dma((2, N)), dma((2, N)), dma((2, N)), dma((2, N)),
             dma((4, N)), dma((4, N)),
         ],

time: 58.7 us -> 52.8 us (0.90)
  Pallas kernels: 58 us -> 52 us
    pallas_call x1, Pallas kernels: 54.6 us -> 48.7 us  [body(): pl.pallas_call(functools.partial(main_kernel, V, S, views), out_shape=(VM...]
where the time goes in v2:
time: 52.8 us; the launch traced here: 52.7 us
  Pallas kernels  52 us (98%)
  between operations  0.64 us (1%)
    pallas_call x1, Pallas kernels, body(): pl.pallas_call(functools.partial(main_kernel, V, S, views), out_shape=(VM...  48.7 us
    pallas_call x1, Pallas kernels, body(): pl.pallas_call(place_kernel, out_shape=(jax.ShapeDtypeStruct((rows, G), f...  3.32 us

profile of v2, /device:TPU:1, one launch (start us, length us, event | category | flops | bytes accessed | tf_op | source)
XLA Modules:
  0.0 52.7 jit_solution(14838596074726785881)
XLA Ops:
  0.6 48.7 %main.1 = (f32[8,128,8,128]{3,2,1,0:T(8,128)S(1)}, f32[256,128]{1,0:T(8,128)S(1)}, s32[8,128]{1,0:T(8,128)S(1)}) custom-call(f32[3,4,3]{2,1,0:T(4,128)} %bitcast.35, f32[4,3]{1,0:T(4,128)} %trns_h.1, f32[4]{0:T(128)} %foc_h.1, s32[128,128]{1,0:T(8,128)} %bitcast.34, f32[128,3,128]{2,1,0:T(4,128)} %bitcast.30, f32[128,3,128]{2,1,0:T(4,128)} %bitcast.31, ...), custom_call_target="tpu_custom_call" | custom-call | tf_op jit(solution)/shard_map/main/pallas_call | solution.py:444
  49.4 3.3 %place.1 = (f32[61,16384]{1,0:T(8,128)}, f32[256,128]{1,0:T(8,128)}, s32[1]{0:T(128)}) custom-call(s32[8,128]{1,0:T(8,128)S(1)} %get-tuple-element.9.idx_v, f32[256,128]{1,0:T(8,128)S(1)} %get-tuple-element.10.peak_in, f32[8,128,8,128]{3,2,1,0:T(8,128)S(1)} %get-tuple-element.11.buf), custom_call_target="tpu_custom_call" | custom-call | tf_op jit(solution)/shard_map/place/pallas_call | solution.py:491

commit v3 on v2

--- a/solution.py
+++ b/solution.py
@@ -57,9 +57,18 @@
     return 0.5 * (a_val + c_val) + disc * lax.rsqrt(disc)
 
 
-YO = (0, 1, 3, 2)
-ZO = (0, 1, 7, 2, 6, 3, 5, 4)
-GROUPS = (2, 2, 4, 8, 8, 8)
+Y, Z = 4, 8
+
+
+def near(step):
+    y, z = (min(a, n - a) for a, n in zip(step, (Y, Z)))
+    return y + z, z
+
+
+STEPS = sorted(((a, b) for a in range(Y) for b in range(Z)), key=near)
+YO, ZO = zip(*STEPS)
+GROUPS = (5, 7, 8, 7, 5)
+LAG = (2, 4)
 
 
 def pick(table, index):
@@ -79,8 +88,6 @@
     v, s = lax.axis_index("view"), lax.axis_index("gauss")
     nblk = mask.shape[0]
     per = nblk // S
-    Z = len(ZO)
-    Y = len(YO)
     X = V // 2
     core = lax.rem(v, 2)
     chip = lax.div(v, 2)
@@ -92,13 +99,18 @@
     i32, f32, bf16 = jnp.int32, jnp.float32, jnp.bfloat16
 
     def dest(p):
-        return lax.rem(y + YO[p // Z], Y) * Z + lax.rem(z + ZO[p % Z], Z)
+        return lax.rem(y + YO[p], Y) * Z + lax.rem(z + ZO[p], Z)
 
     bar = pltpu.get_barrier_semaphore()
     for p in range(1, S):
         pl.semaphore_signal(bar, inc=1, device_id=peer(v, dest(p)), device_id_type=MESH)
     for to in (mate, nxt, prv, opp):
         pl.semaphore_signal(bar, inc=1, device_id=peer(to, s), device_id_type=MESH)
+
+    @pl.when(v == V - 1)
+    def _():
+        for k in range(X - 1):
+            pl.semaphore_signal(bar, inc=1, device_id=peer(2 * k, s), device_id_type=MESH)
 
     loads = [
         pltpu.make_async_copy(a, b, lsem.at[i])
@@ -180,14 +192,14 @@
         started.append(copy)
         return copy
 
-    pl.semaphore_wait(bar, S + 3)
+    pl.semaphore_wait(bar, S + 3 + jnp.where((core == 0) & (chip < X - 1), 1, 0))
     tally = [
         go(remote(cnt, counts.at[pl.ds(p, 1), :], csend.at[p], crecv.at[p], peer(v, dest(p))))
-        for p in range(1, S)
+        for p in reversed(range(1, S))
     ]
     mine = pl.ds(pl.multiple_of(core * nblk, nblk), nblk)
-    other = pl.ds(pl.multiple_of((1 - core) * nblk, nblk), nblk)
-    pair = go(remote(local.at[other, :], halves, psend.at[0], precv.at[0], peer(mate, s)))
+    last = V - 1
+    pair = go(remote(local, halves, psend.at[0], precv.at[0], peer(mate, s)))
     counts[0:1, :] = cnt[...]
 
     lane = lax.broadcasted_iota(i32, (nblk, LANES), 1)
@@ -222,11 +234,14 @@
 
 
     pair.wait_recv()
-    merged[...] = jnp.maximum(local[mine, :], halves[...])
-    spread = [
-        go(remote(merged, whole.at[k], psend.at[1 + k], precv.at[1 + k], peer(to, s)))
-        for k, to in enumerate((nxt, prv, opp))
-    ]
+    merged[...] = jnp.maximum(local[...], halves[...])
+    spread = []
+    for k in range(1, X):
+        to = lax.rem(chip + k, X)
+        spread.append(go(remote(
+            merged.at[mine, :], whole.at[k - 1, mine, :], psend.at[k], precv.at[k + X * core],
+            peer(2 * to + jnp.where(to == X - 1, 1, core), s),
+        )))
 
     tiles(lambda c: c.wait())
 
@@ -277,18 +292,20 @@
         for c in finals:
             packed[:, c, :] = moved[:, (c - lo) * LANES:(c - lo + 1) * LANES]
 
-    full = remote(peak.at[mine, :], peak.at[mine, :], psend.at[4], precv.at[4], peer(mate, s))
-
-    def finish():
-        for c in spread:
-            c.wait_recv()
-        best = merged[...]
-        for k in range(3):
-            best = jnp.maximum(best, whole[k])
+    full = remote(peak.at[mine, :], peak.at[mine, :], psend.at[X + 1], precv.at[X], peer(mate, s))
+    extra = remote(peak, peak, psend.at[X], precv.at[X], peer(mate, s))
+
+    def arrive(half):
+        for k in range(1, X):
+            ref = whole.at[k - 1, pl.ds(half * nblk, nblk), :]
+            remote(ref, ref, psend.at[k], precv.at[k + X * half], peer(mate, s)).wait_recv()
+
+    def finish(rows):
+        best = merged[rows, :]
+        for k in range(X - 1):
+            best = jnp.maximum(best, whole[k, rows, :])
         odd = (lax.broadcasted_iota(i32, best.shape, 0) & 1) == 1
-        peak[mine, :] = jnp.sqrt(best) * jnp.where(odd, 3.0, 1.0)
-        full.start()
-        full.wait_recv()
+        peak[rows, :] = jnp.sqrt(best) * jnp.where(odd, 3.0, 1.0)
 
     pack(0, 1, 2)
 
@@ -299,13 +316,16 @@
     @pl.when(v == TILES - 1)
     def _():
         packed[:, 5:, :] = jnp.zeros((nblk, 3, LANES), f32)
-        finish()
+        arrive(0)
+        arrive(1)
+        finish(pl.ds(0, 2 * nblk))
+        extra.start()
         for c in range(2):
             put(3 + c, peak[pl.ds(c, nblk, stride=2), :])
         pack(3, 4)
 
     def source(p):
-        return ((y - pick(YO, p >> 3)) & (Y - 1)) * Z + ((z - pick(ZO, p & 7)) & (Z - 1))
+        return ((y - pick(YO, p)) & (Y - 1)) * Z + ((z - pick(ZO, p)) & (Z - 1))
 
     p32 = lax.broadcasted_iota(i32, (S, LANES), 0)
     lower = source(p32) < s
@@ -328,11 +348,22 @@
     own = pltpu.make_async_copy(send.at[pl.ds(0, per)], buf.at[v, pl.ds(0, per)], fsend.at[0])
     own.start()
 
-    @pl.when(v < TILES - 1)
-    def _():
-        finish()
-
-    started.append(full)
+    for half in range(2):
+        @pl.when((chip < X - 1) & (core == half))
+        def _():
+            arrive(half)
+            finish(mine)
+            full.start()
+            full.wait()
+
+    @pl.when(v == last - 1)
+    def _():
+        extra.wait_recv()
+
+    @pl.when(v == last)
+    def _():
+        extra.wait_send()
+
     pr = lax.broadcasted_iota(i32, (S, S), 0)
     pc = lax.broadcasted_iota(i32, (S, S), 1)
     less = (source(pc) < source(pr)).astype(bf16)
@@ -369,7 +400,7 @@
         return remote(ref, ref, msend.at[q, i], mrecv.at[q, i], peer(mate, s))
 
     rings, relays, besides = {}, {}, {}
-    for i in range(N + 2):
+    for i in range(N + LAG[1]):
         if i < N:
             for p in range(edges[i], edges[i + 1]):
                 if p:
@@ -379,15 +410,18 @@
             for way in range(2):
                 rings[i, way] = go(ring(i, way))
             besides[i, 0] = go(beside(i, 0))
-        if 1 <= i <= N:
+        j = i - LAG[0]
+        if 0 <= j < N:
             for way in range(2):
-                rings[i - 1, way].wait_recv()
-                relays[i - 1, way] = go(relay(i - 1, way))
-                besides[i - 1, 1 + way] = go(beside(i - 1, 1 + way))
-        if i >= 2:
+                rings[j, way].wait_recv()
+                relays[j, way] = go(relay(j, way))
             for way in range(2):
-                relays[i - 2, way].wait_recv()
-            besides[i - 2, 3] = go(beside(i - 2, 3))
+                besides[j, 1 + way] = go(beside(j, 1 + way))
+        j = i - LAG[1]
+        if 0 <= j < N:
+            for way in range(2):
+                relays[j, way].wait_recv()
+            besides[j, 3] = go(beside(j, 3))
     for c in besides.values():
         c.wait_recv()
     for c in started:
@@ -468,10 +502,10 @@
             VMEM((1, LANES), i32),
             VMEM((S, LANES), i32),
             VMEM((2 * nblk, LANES), f32),
-            VMEM((nblk, LANES), f32),
-            VMEM((nblk, LANES), f32),
-            VMEM((3, nblk, LANES), f32),
-            dma((11,)), dma((S,)), dma((S,)), dma((5,)), dma((5,)),
+            VMEM((2 * nblk, LANES), f32),
+            VMEM((2 * nblk, LANES), f32),
+            VMEM((V // 2 - 1, 2 * nblk, LANES), f32),
+            dma((11,)), dma((S,)), dma((S,)), dma((V,)), dma((V,)),
             dma((S,)), dma((S,)), dma((2, N)), dma((2, N)), dma((2, N)), dma((2, N)),
             dma((4, N)), dma((4, N)),
         ],

time: 52.8 us -> 49.4 us (0.936)
  Pallas kernels: 52 us -> 48.6 us
    pallas_call x1, Pallas kernels: 48.7 us -> 45.3 us  [body(): pl.pallas_call(functools.partial(main_kernel, V, S, views), out_shape=(VM...]
where the time goes in v3:
time: 49.4 us; the launch traced here: 49.3 us
  Pallas kernels  48.6 us (98%)
  between operations  0.64 us (1%)
    pallas_call x1, Pallas kernels, body(): pl.pallas_call(functools.partial(main_kernel, V, S, views), out_shape=(VM...  45.3 us
    pallas_call x1, Pallas kernels, body(): pl.pallas_call(place_kernel, out_shape=(jax.ShapeDtypeStruct((rows, G), f...  3.32 us

profile of v3, /device:TPU:1, one launch (start us, length us, event | category | flops | bytes accessed | tf_op | source)
XLA Modules:
  0.0 49.3 jit_solution(7354243787835737151)
XLA Ops:
  0.6 45.3 %main.1 = (f32[8,128,8,128]{3,2,1,0:T(8,128)S(1)}, f32[256,128]{1,0:T(8,128)S(1)}, s32[8,128]{1,0:T(8,128)S(1)}) custom-call(f32[3,4,3]{2,1,0:T(4,128)} %bitcast.35, f32[4,3]{1,0:T(4,128)} %trns_h.1, f32[4]{0:T(128)} %foc_h.1, s32[128,128]{1,0:T(8,128)} %bitcast.34, f32[128,3,128]{2,1,0:T(4,128)} %bitcast.30, f32[128,3,128]{2,1,0:T(4,128)} %bitcast.31, ...), custom_call_target="tpu_custom_call" | custom-call | tf_op jit(solution)/shard_map/main/pallas_call | solution.py:478
  45.9 3.3 %place.1 = (f32[61,16384]{1,0:T(8,128)}, f32[256,128]{1,0:T(8,128)}, s32[1]{0:T(128)}) custom-call(s32[8,128]{1,0:T(8,128)S(1)} %get-tuple-element.9.idx_v, f32[256,128]{1,0:T(8,128)S(1)} %get-tuple-element.10.peak_in, f32[8,128,8,128]{3,2,1,0:T(8,128)S(1)} %get-tuple-element.11.buf), custom_call_target="tpu_custom_call" | custom-call | tf_op jit(solution)/shard_map/place/pallas_call | solution.py:525

commit v4 on v3

--- a/solution.py
+++ b/solution.py
@@ -69,6 +69,7 @@
 YO, ZO = zip(*STEPS)
 GROUPS = (5, 7, 8, 7, 5)
 LAG = (2, 4)
+SETTLE = 1
 
 
 def pick(table, index):
@@ -81,7 +82,7 @@
 def main_kernel(
     V, S, views, rots_h, trns_h, foc_h, mask_h, means_h, scales_h, quats_h, attrs_h, grad_h, vis_h,
     buf, peak, where_out,
-    rots, trns, foc, mask, means, scales, quats, grad, vis, fac, x, enc, g, split, packed, send, cnt, counts,
+    rots, trns, foc, mask, means, scales, quats, grad, vis, fac, x, enc, g, split, packed, send, found_v, cnt, counts,
     local, halves, merged, whole, lsem, csend, crecv, psend, precv,
     fsend, frecv, xsend, xrecv, hsend, hrecv, msend, mrecv,
 ):
@@ -348,21 +349,13 @@
     own = pltpu.make_async_copy(send.at[pl.ds(0, per)], buf.at[v, pl.ds(0, per)], fsend.at[0])
     own.start()
 
-    for half in range(2):
-        @pl.when((chip < X - 1) & (core == half))
-        def _():
-            arrive(half)
-            finish(mine)
-            full.start()
-            full.wait()
-
-    @pl.when(v == last - 1)
-    def _():
-        extra.wait_recv()
-
-    @pl.when(v == last)
-    def _():
-        extra.wait_send()
+    def settle():
+        for half in range(2):
+            @pl.when((chip < X - 1) & (core == half))
+            def _():
+                arrive(half)
+                finish(mine)
+                full.start()
 
     pr = lax.broadcasted_iota(i32, (S, S), 0)
     pc = lax.broadcasted_iota(i32, (S, S), 1)
@@ -374,7 +367,9 @@
     found = jnp.sum(spot, axis=0, keepdims=True) - 1
     total = jnp.sum(tot, axis=0, keepdims=True)
     sub = lax.broadcasted_iota(i32, (SUB, LANES), 0)
-    where_out[...] = jnp.where(sub == 0, found, total)
+    found_v[...] = jnp.where(sub == 0, found, total)
+    tell = pltpu.make_async_copy(found_v, where_out, lsem.at[0])
+    tell.start()
 
     edges = [0]
     for n in GROUPS:
@@ -410,6 +405,8 @@
             for way in range(2):
                 rings[i, way] = go(ring(i, way))
             besides[i, 0] = go(beside(i, 0))
+        if i == SETTLE:
+            settle()
         j = i - LAG[0]
         if 0 <= j < N:
             for way in range(2):
@@ -422,21 +419,31 @@
             for way in range(2):
                 relays[j, way].wait_recv()
             besides[j, 3] = go(beside(j, 3))
+    @pl.when(chip < X - 1)
+    def _():
+        full.wait()
+
+    @pl.when(v == last - 1)
+    def _():
+        extra.wait_recv()
+
+    @pl.when(v == last)
+    def _():
+        extra.wait_send()
+
+    tell.wait()
     for c in besides.values():
         c.wait_recv()
     for c in started:
         c.wait_send()
 
 
-def place_kernel(idx_v, peak_in, buf, clones, peak, total, out, idx, isem, osem, psem):
+def place_kernel(idx, peak_in, buf, clones, peak, total, out, osem, psem):
     rows = clones.shape[0]
     slots = out.shape[1] // LANES
     chunks = osem.shape[0]
-    fetch = pltpu.make_async_copy(idx_v, idx, isem)
-    fetch.start()
     top = pltpu.make_async_copy(peak_in, peak, psem)
     top.start()
-    fetch.wait()
     total[0] = idx[1, 0]
     each = slots // chunks
     outs = []
@@ -478,10 +485,10 @@
     buf, peak, where = pl.pallas_call(
         functools.partial(main_kernel, V, S, views),
         out_shape=(
-            VMEM((V, nblk, SUB, LANES), f32), VMEM((2 * nblk, LANES), f32), VMEM((SUB, LANES), i32),
+            VMEM((V, nblk, SUB, LANES), f32), VMEM((2 * nblk, LANES), f32), SMEM((SUB, LANES), i32),
         ),
         in_specs=[spec(HBM)] * 10,
-        out_specs=(spec(VMEM),) * 3,
+        out_specs=(spec(VMEM), spec(VMEM), spec(SMEM)),
         scratch_shapes=[
             SMEM((3, views, 3), f32),
             SMEM((views, 3), f32),
@@ -499,6 +506,7 @@
             VMEM((6 * nblk, SUB * LANES), jnp.bfloat16),
             VMEM((nblk, SUB, LANES), f32),
             VMEM((nblk, SUB, LANES), f32),
+            VMEM((SUB, LANES), i32),
             VMEM((1, LANES), i32),
             VMEM((S, LANES), i32),
             VMEM((2 * nblk, LANES), f32),
@@ -529,9 +537,9 @@
             jax.ShapeDtypeStruct((2 * nblk, LANES), f32),
             jax.ShapeDtypeStruct((1,), i32),
         ),
-        in_specs=[spec(VMEM)] * 3,
+        in_specs=[spec(SMEM), spec(VMEM), spec(VMEM)],
         out_specs=(spec(pl.ANY), spec(pl.ANY), spec(SMEM)),
-        scratch_shapes=[VMEM((rows, G), f32), SMEM((SUB, LANES), i32), dma, dma((chunks,)), dma],
+        scratch_shapes=[VMEM((rows, G), f32), dma((chunks,)), dma],
         compiler_params=pltpu.CompilerParams(vmem_limit_bytes=limit),
         name="place",
     )(where, peak, buf)

time: 49.4 us -> 48.7 us (0.986)
  Pallas kernels: 48.6 us -> 48 us
    pallas_call x1, Pallas kernels: 3.32 us -> 2.72 us  [body(): pl.pallas_call(place_kernel, out_shape=(jax.ShapeDtypeStruct((rows, G), f...]
where the time goes in v4:
time: 48.7 us; the launch traced here: 48.6 us
  Pallas kernels  48 us (99%)
  between operations  0.64 us (1%)
    pallas_call x1, Pallas kernels, body(): pl.pallas_call(functools.partial(main_kernel, V, S, views), out_shape=(VM...  45.3 us
    pallas_call x1, Pallas kernels, body(): pl.pallas_call(place_kernel, out_shape=(jax.ShapeDtypeStruct((rows, G), f...  2.72 us

profile of v4, /device:TPU:1, one launch (start us, length us, event | category | flops | bytes accessed | tf_op | source)
XLA Modules:
  0.0 48.6 jit_solution(5059190148624595249)
XLA Ops:
  0.6 45.3 %main.1 = (f32[8,128,8,128]{3,2,1,0:T(8,128)S(1)}, f32[256,128]{1,0:T(8,128)S(1)}, s32[8,128]{1,0:T(8,128)S(4)}) custom-call(f32[3,4,3]{2,1,0:T(4,128)} %bitcast.35, f32[4,3]{1,0:T(4,128)} %trns_h.1, f32[4]{0:T(128)} %foc_h.1, s32[128,128]{1,0:T(8,128)} %bitcast.34, f32[128,3,128]{2,1,0:T(4,128)} %bitcast.30, f32[128,3,128]{2,1,0:T(4,128)} %bitcast.31, ...), custom_call_target="tpu_custom_call" | custom-call | tf_op jit(solution)/shard_map/main/pallas_call | solution.py:485
  45.9 2.7 %place.1 = (f32[61,16384]{1,0:T(8,128)}, f32[256,128]{1,0:T(8,128)}, s32[1]{0:T(128)}) custom-call(s32[8,128]{1,0:T(8,128)S(4)} %get-tuple-element.9.idx, f32[256,128]{1,0:T(8,128)S(1)} %get-tuple-element.10.peak_in, f32[8,128,8,128]{3,2,1,0:T(8,128)S(1)} %get-tuple-element.11.buf), custom_call_target="tpu_custom_call" | custom-call | tf_op jit(solution)/shard_map/place/pallas_call | solution.py:533

commit v5 on v4

--- a/solution.py
+++ b/solution.py
@@ -395,6 +395,8 @@
         return remote(ref, ref, msend.at[q, i], mrecv.at[q, i], peer(mate, s))
 
     rings, relays, besides = {}, {}, {}
+    done = set()
+    marks = {N - 1: len(started)}
     for i in range(N + LAG[1]):
         if i < N:
             for p in range(edges[i], edges[i + 1]):
@@ -407,6 +409,9 @@
             besides[i, 0] = go(beside(i, 0))
         if i == SETTLE:
             settle()
+        for c in started[:marks.get(i, 0)]:
+            c.wait_send()
+            done.add(id(c))
         j = i - LAG[0]
         if 0 <= j < N:
             for way in range(2):
@@ -435,7 +440,8 @@
     for c in besides.values():
         c.wait_recv()
     for c in started:
-        c.wait_send()
+        if id(c) not in done:
+            c.wait_send()
 
 
 def place_kernel(idx, peak_in, buf, clones, peak, total, out, osem, psem):

time: 48.7 us -> 48.6 us (level)
  no operation moved by 1% of the time
where the time goes in v5:
time: 48.6 us; the launch traced here: 48.5 us
  Pallas kernels  47.9 us (99%)
  between operations  0.64 us (1%)
    pallas_call x1, Pallas kernels, body(): pl.pallas_call(functools.partial(main_kernel, V, S, views), out_shape=(VM...  45.2 us
    pallas_call x1, Pallas kernels, body(): pl.pallas_call(place_kernel, out_shape=(jax.ShapeDtypeStruct((rows, G), f...  2.72 us

profile of v5, /device:TPU:1, one launch (start us, length us, event | category | flops | bytes accessed | tf_op | source)
XLA Modules:
  0.0 48.5 jit_solution(1952540235179808417)
XLA Ops:
  0.6 45.2 %main.1 = (f32[8,128,8,128]{3,2,1,0:T(8,128)S(1)}, f32[256,128]{1,0:T(8,128)S(1)}, s32[8,128]{1,0:T(8,128)S(4)}) custom-call(f32[3,4,3]{2,1,0:T(4,128)} %bitcast.35, f32[4,3]{1,0:T(4,128)} %trns_h.1, f32[4]{0:T(128)} %foc_h.1, s32[128,128]{1,0:T(8,128)} %bitcast.34, f32[128,3,128]{2,1,0:T(4,128)} %bitcast.30, f32[128,3,128]{2,1,0:T(4,128)} %bitcast.31, ...), custom_call_target="tpu_custom_call" | custom-call | tf_op jit(solution)/shard_map/main/pallas_call | solution.py:491
  45.8 2.7 %place.1 = (f32[61,16384]{1,0:T(8,128)}, f32[256,128]{1,0:T(8,128)}, s32[1]{0:T(128)}) custom-call(s32[8,128]{1,0:T(8,128)S(4)} %get-tuple-element.9.idx, f32[256,128]{1,0:T(8,128)S(1)} %get-tuple-element.10.peak_in, f32[8,128,8,128]{3,2,1,0:T(8,128)S(1)} %get-tuple-element.11.buf), custom_call_target="tpu_custom_call" | custom-call | tf_op jit(solution)/shard_map/place/pallas_call | solution.py:539
